TPU v7x, 32 devices: a whole 2x2x4 slice. The times are simulated.
32 devices in a mesh: hist: 16 (over z, x, core), orb: 2 (over y).
Axes of the slice: x: 2, y: 2, z: 4, core: 2. Of those that a mesh axis runs over, the one named last changes fastest.
Arguments:
- g_hist: bfloat16 [32, 64, 2048], P('hist', 'orb'), may hold values from -6 to 6
- sigma_hist: bfloat16 [2, 64, 2048], P(None, None, 'hist'), may hold values from -0.125 to 0.125
- diag_inv: float32 [32, 64, 64], P('hist'), may hold values from -0.75 to 0.75
- previous: float32 [2, 32, 64, 64], P(None, 'hist', 'orb'), may hold values from -6 to 6
- block_of_slot: int32 [16], replicated, may hold values from 0 to 15, each once
- front_pos: int32 [2], replicated, may hold values from 16 to 31
Outputs:
- g_row: float32 [2, 32, 64, 64], P(None, 'hist', 'orb')
- sigma_row: float32 [2, 32, 64, 64], P(None, 'hist', 'orb')
Inputs may be any that keep to these rules, and one draw needn't show every extreme that they name: `block_of_slot`: every block index appears once.
All inputs are finite; a program needn't handle non-finite values.
Results may differ from a plain program's by a relative error of at most 0.0003.
Values may be sent and summed in bfloat16 or wider, within the bound.
A program may use at most 64 MiB of HBM per device.

v0:
```python
import functools

import jax
import jax.numpy as jnp
from jax import lax
from jax.experimental import pallas as pl
from jax.experimental.pallas import tpu as pltpu
from jax.sharding import PartitionSpec as P

COUPLING = 0.5
MESH = pl.DeviceIdType.MESH


def xor(a, b, size):
    out, bit = 0, 1
    while bit < size:
        out = out + bit * ((a // bit + b // bit) % 2)
        bit *= 2
    return out


def loop(low, high, step):
    if high - low <= 8:
        for i in range(low, high):
            step(i)
    else:
        lax.fori_loop(low, high, lambda i, c: (step(i), c)[1], 0)


def kernel(lines, blocks_ref, front_ref, g_hbm, s_hbm, d_hbm, p_hbm, out,
           g_v, all_s, d_v, p_v, acc, d_out, d_in, d_z, d_all, packed,
           loc_sem, z_send, z_recv, x_send, x_recv, c_send, c_recv,
           d_send, d_recv, dz_send, dz_recv, y_send, y_recv):
    cols, half = g_hbm.shape[0], g_hbm.shape[1]
    orb, lanes = s_hbm.shape[1], s_hbm.shape[2]
    me = lax.axis_index("hist")
    o = lax.axis_index("orb")
    core = me % 2
    xi = (me // 2) % 2
    z = me // 4
    rows = orb // 2

    def at(zz, xx, cc):
        return (zz * 2 + xx) * 2 + cc

    core_peer = (at(z, xi, 1 - core), o)
    x_peer = (at(z, 1 - xi, core), o)
    xc_peer = (at(z, 1 - xi, 1 - core), o)
    y_peer = (me, 1 - o)

    def z_peer(d):
        return (at(xor(z, d, lines), xi, core), o)

    load_s = pltpu.make_async_copy(s_hbm.at[o], all_s.at[z, xi, core], loc_sem.at[0])
    load_d = pltpu.make_async_copy(d_hbm, d_v, loc_sem.at[1])
    load_g = pltpu.make_async_copy(g_hbm, g_v.at[o], loc_sem.at[2])
    load_p = pltpu.make_async_copy(p_hbm.at[o], p_v.at[o], loc_sem.at[3])
    load_s.start()
    load_d.start()
    load_g.start()
    load_p.start()

    barrier = pltpu.get_barrier_semaphore()

    def greet(peer):
        pl.semaphore_signal(barrier, inc=1, device_id=peer, device_id_type=MESH)

    loop(1, lines, lambda d: greet(z_peer(d)))
    for peer in (x_peer, xc_peer, core_peer, y_peer):
        greet(peer)

    def rows_of(part):
        when = front_ref[o]
        mine = (when // cols) == me
        first = pl.multiple_of(part * rows, 8)
        got = d_v[when % cols, pl.ds(first, rows), :]
        wide = jnp.concatenate([got[:rows // 2], got[rows // 2:]], axis=1)
        return jnp.where(mine, wide, jnp.zeros_like(wide))

    load_d.wait()
    d_out[0] = rows_of(core)
    d_out[1] = rows_of(1 - core)
    acc[...] = jnp.zeros_like(acc)
    load_s.wait()
    pl.semaphore_wait(barrier, lines + 3)

    def send(src, dst, ssem, rsem, peer):
        return pltpu.make_async_remote_copy(
            src_ref=src, dst_ref=dst, send_sem=ssem, recv_sem=rsem,
            device_id=peer, device_id_type=MESH)

    def piece(d, xx, cc):
        return all_s.at[xor(z, d, lines), xx, cc]

    def z_copy(d):
        return send(piece(0, xi, core), piece(0, xi, core), z_send.at[d], z_recv.at[d], z_peer(d))

    def x_copy(d):
        return send(piece(d, xi, core), piece(d, xi, core), x_send.at[d], x_recv.at[d], x_peer)

    def c_copy(d, other):
        xx = xi + other - 2 * xi * other
        k = other * lines + d
        return send(piece(d, xx, core), piece(d, xx, core), c_send.at[k], c_recv.at[k], core_peer)

    d_copies = [send(d_out.at[which], d_in.at[k], d_send.at[k], d_recv.at[k], peer)
                for k, (which, peer) in enumerate(((0, x_peer), (1, xc_peer), (1, core_peer)))]
    for c in d_copies:
        c.start()
    x_copy(0).start()
    loop(1, lines, lambda d: z_copy(lines - d).start())
    c_copy(0, 0).start()
    load_g.wait()
    g_copy = send(g_v.at[o], g_v.at[o], y_send.at[0], y_recv.at[0], y_peer)
    p_copy = send(p_hbm.at[1 - o], p_v.at[o], y_send.at[1], y_recv.at[1], y_peer)
    g_copy.start()
    p_copy.start()

    col0 = blocks_ref[me] * cols

    def product(d, xx):
        zz = xor(z, d, lines)
        width = 2 * lanes
        start = pl.multiple_of((zz * 2 + xx) * width, width)
        time = (lax.broadcasted_iota(jnp.int32, (1, width), 1) + start) // orb
        one, zero = jnp.float32(1), jnp.float32(0)
        left = []
        for t in range(cols):
            keep = jnp.where((time >= col0 + t) & (time <= front_ref[o]), one, zero)
            keep = keep.astype(jnp.bfloat16)
            left += [g_v[h, t, :, pl.ds(start, width)] * keep for h in range(2)]
        right = jnp.concatenate([all_s[zz, xx, 0], all_s[zz, xx, 1]], axis=1)
        acc[...] += lax.dot_general(jnp.concatenate(left, axis=0), right, (((1,), (1,)), ((), ())),
                                    preferred_element_type=jnp.float32)

    def relay(d):
        z_copy(d).wait_recv()
        x_copy(d).start()
        c_copy(d, 0).start()

    def relay_x(d):
        x_copy(d).wait_recv()
        c_copy(d, 1).start()

    def near(d):
        c_copy(d, 0).wait_recv()
        product(d, xi)

    def far(d):
        c_copy(d, 1).wait_recv()
        product(d, 1 - xi)

    def dz_copy(d):
        return send(d_z.at[0], d_z.at[d], dz_send.at[d], dz_recv.at[d], z_peer(d))

    relay_x(0)
    for c in d_copies:
        c.wait()
    d_z[0] = (d_out[0] + d_in[0]) + (d_in[1] + d_in[2])
    loop(1, lines, lambda d: dz_copy(d).start())
    loop(1, lines, relay)
    loop(1, lines - 1, relay_x)
    g_copy.wait_recv()
    near(0)
    near(1)
    relay_x(lines - 1)
    loop(1, lines, lambda d: dz_copy(d).wait())
    total = lax.fori_loop(1, lines, lambda d, t: t + d_z[d], d_z[0])
    d_all[core] = total
    d_last = send(d_all.at[core], d_all.at[core], d_send.at[3], d_recv.at[3], core_peer)
    d_last.start()
    loop(2, lines, near)
    loop(0, lines, far)

    load_p.wait()
    p_copy.wait()
    prev = jnp.concatenate([p_v[h, t] for t in range(cols) for h in range(2)], axis=0)
    combined = acc[...] + prev
    d_last.wait()
    weight = jnp.concatenate([d_all[c][:, k * orb:(k + 1) * orb]
                              for c in range(2) for k in range(2)], axis=0)
    contract = (((1,), (1,)), ((), ()))
    high = dict(precision=lax.Precision.HIGHEST, preferred_element_type=jnp.float32)
    flipped = lax.dot_general(weight, combined, contract, **high)
    g_new = lax.dot_general(combined, weight, contract, **high)
    t_copies = []
    for t in range(cols):
        g_t = g_new[t * orb:(t + 1) * orb]
        s_t = COUPLING * g_t * g_t * flipped[:, t * orb:(t + 1) * orb]
        done = jnp.concatenate([g_t, s_t], axis=1)
        packed[t] = jnp.where(o == 0, done[half:], done[:half])
        c = send(packed.at[t], out.at[o, t], y_send.at[2 + t], y_recv.at[2 + t], y_peer)
        c.start()
        t_copies.append(c)
        out[o, t] = jnp.where(o == 0, done[:half], done[half:])

    g_copy.wait_send()
    loop(1, lines, lambda d: z_copy(d).wait_send())
    loop(0, lines, lambda d: x_copy(d).wait_send())
    loop(0, lines, lambda d: c_copy(d, 0).wait_send())
    loop(0, lines, lambda d: c_copy(d, 1).wait_send())
    for c in t_copies:
        c.wait()


def body(lines, g_hist, sigma_hist, diag_inv, previous, block_of_slot, front_pos):
    cols, half, depth = g_hist.shape
    orb, lanes = sigma_hist.shape[1], sigma_hist.shape[2]
    smem = pl.BlockSpec(memory_space=pltpu.SMEM)
    hbm = pl.BlockSpec(memory_space=pl.ANY)
    dma = pltpu.SemaphoreType.DMA
    f32 = jnp.float32
    part = (orb // 4, 2 * orb)
    flops = 2 * cols * orb * depth * orb
    out = pl.pallas_call(
        functools.partial(kernel, lines),
        out_shape=pltpu.VMEM((2, cols, half, 2 * orb), f32),
        in_specs=[smem, smem, hbm, hbm, hbm, hbm],
        out_specs=pl.BlockSpec(memory_space=pltpu.VMEM),
        scratch_shapes=[
            pltpu.VMEM((2,) + g_hist.shape, g_hist.dtype),
            pltpu.VMEM((lines, 2, 2, orb, lanes), sigma_hist.dtype),
            pltpu.VMEM(diag_inv.shape, f32),
            pltpu.VMEM((2,) + previous.shape[1:], f32),
            pltpu.VMEM((cols * orb, orb), f32),
            pltpu.VMEM((2,) + part, f32),
            pltpu.VMEM((3,) + part, f32),
            pltpu.VMEM((lines,) + part, f32),
            pltpu.VMEM((2,) + part, f32),
            pltpu.VMEM((cols, half, 2 * orb), f32),
            dma((4,)),
            dma((lines,)), dma((lines,)),
            dma((lines,)), dma((lines,)),
            dma((2 * lines,)), dma((2 * lines,)),
            dma((4,)), dma((4,)),
            dma((lines,)), dma((lines,)),
            dma((2 + cols,)), dma((2 + cols,)),
        ],
        compiler_params=pltpu.CompilerParams(collective_id=0, has_side_effects=True),
        cost_estimate=pl.CostEstimate(flops=flops, bytes_accessed=2 * g_hist.size, transcendentals=0),
    )(block_of_slot, front_pos, g_hist, sigma_hist, diag_inv, previous)
    return out[..., :orb], out[..., orb:]


def solution(mesh):
    lines = mesh.shape["hist"] // 4
    in_specs = (
        P("hist", "orb", None),
        P(None, None, "hist"),
        P("hist", None, None),
        P(None, "hist", "orb", None),
        P(),
        P(),
    )
    out_specs = (P(None, "hist", "orb", None), P(None, "hist", "orb", None))
    return jax.shard_map(functools.partial(body, lines), mesh=mesh, in_specs=in_specs,
                         out_specs=out_specs, check_vma=False)
```

profile of v0, /device:TPU:0, one launch (start us, length us, event | category | flops | bytes accessed | tf_op | source)
XLA Modules:
  0.0 19.8 jit_solution(11294096367925441126)
XLA Ops:
  0.6 18.5 %shard_map.77 = f32[2,2,32,128]{3,2,1,0:T(8,128)S(1)} custom-call(s32[16]{0:T(128)} %blocks_ref.1, s32[2]{0:T(128)} %front_ref.1, bf16[2,32,2048]{2,1,0:T(8,128)(2,1)} %g_hbm.1, bf16[2,64,128]{2,1,0:T(8,128)(2,1)} %s_hbm.1, f32[2,64,64]{2,1,0:T(8,128)} %d_hbm.1, f32[2,2,32,64]{3,2,1,0:T(8,128)} %p_hbm.1), custom_call_target="tpu_custom_call" | custom-call | flops 33554432 | bytes 262144 | tf_op jit(solution)/shard_map/pallas_call | solution.py:215
  19.1 0.7 %fusion = (f32[2,2,32,64]{3,2,1,0:T(8,128)}, f32[2,2,32,64]{3,2,1,0:T(8,128)}) fusion(f32[2,2,32,128]{3,2,1,0:T(8,128)S(1)} %shard_map.77), kind=kLoop, calls=%fused_computation | loop fusion | bytes 131072 | tf_op jit(solution)/shard_map/slice | solution.py:242
where the time goes:
time: 20 us; the launch traced here: 19.8 us
  Pallas kernels  18.5 us (92%)
  local copies, waits for them, and re-layouts  0.72 us (4%)
  between operations  0.64 us (3%)
    pallas_call x1, Pallas kernels, body(): pl.pallas_call(functools.partial(kernel, lines), out_shape=pltpu.VMEM((2,...  18.5 us
    slice x1, local copies, waits for them, and re-layouts, body(): return (out[..., :orb], out[..., orb:])  0.72 us

commit v1 on v0

v1 whole, which is shorter than its diff:
```python
import functools

import jax
import jax.numpy as jnp
from jax import lax
from jax.experimental import pallas as pl
from jax.experimental.pallas import tpu as pltpu
from jax.sharding import PartitionSpec as P

COUPLING = 0.5
MESH = pl.DeviceIdType.MESH


def xor(a, b, size):
    out, bit = 0, 1
    while bit < size:
        out = out + bit * ((a // bit + b // bit) % 2)
        bit *= 2
    return out


def loop(low, high, step):
    if high - low <= 8:
        for i in range(low, high):
            step(i)
    else:
        lax.fori_loop(low, high, lambda i, c: (step(i), c)[1], 0)


def split(x):
    high = x.astype(jnp.bfloat16)
    return high, (x - high.astype(jnp.float32)).astype(jnp.bfloat16)


def kernel(lines, blocks_hbm, front_hbm, g_hbm, s_hbm, d_hbm, p_hbm, out,
           blocks, front, g_v, all_s, d_v, p_v, acc, part, total,
           loc, s_send, s_recv, c_send, c_recv, e_send, e_recv, t_send, t_recv,
           y_send, y_recv, ready, s_ready):
    cols, half = g_hbm.shape[0], g_hbm.shape[1]
    fronts, orb, lanes = s_hbm.shape
    me = lax.axis_index("hist")
    o = lax.axis_index("orb")
    core = me % 2
    xi = (me // 2) % 2
    z = me // 4

    def at(zz, xx, cc):
        return (zz * 2 + xx) * 2 + cc

    def scope(name):
        return jax.named_scope(name)

    y_peer = (me, 1 - o)
    core_peer = (at(z, xi, 1 - core), o)
    xc_peer = (at(z, 1 - xi, 1 - core), o)
    near = ((y_peer, o), (core_peer, core), (xc_peer, xi))

    def peer_at(zz, xx):
        return (at(zz, xx, core), o)

    def flip(bit, k):
        return bit + k - 2 * bit * k

    def slot(zz, xx):
        return flip(xi, xx) * lines + xor(zz, z, lines)

    barrier = pltpu.get_barrier_semaphore()

    def signal(sem, peer):
        pl.semaphore_signal(sem, inc=1, device_id=peer, device_id_type=MESH)

    def uppers(step):
        @pl.when(xi == 0)
        def _():
            step(z, 1)

        def one(zz):
            @pl.when(zz > z)
            def _():
                step(zz, 0)
                step(zz, 1)

        loop(1, lines, one)

    def lowers(step):
        def one(zz):
            @pl.when(zz < z)
            def _():
                step(zz, 0)
                step(zz, 1)

        loop(0, lines - 1, one)

        @pl.when(xi == 1)
        def _():
            step(z, 0)

    for peer, upper in near:
        @pl.when(upper == 0)
        def _():
            signal(barrier, peer)

    uppers(lambda zz, xx: signal(barrier, peer_at(zz, xx)))

    load_f = pltpu.make_async_copy(front_hbm, front, loc.at[5])
    load_d = pltpu.make_async_copy(d_hbm, d_v, loc.at[1])
    load_s = pltpu.make_async_copy(s_hbm, all_s.at[z, xi, core], loc.at[0])
    load_g = pltpu.make_async_copy(g_hbm, g_v.at[o], loc.at[2])
    load_p = pltpu.make_async_copy(p_hbm, p_v.at[o], loc.at[3])
    load_b = pltpu.make_async_copy(blocks_hbm, blocks, loc.at[4])
    load_f.start()
    load_d.start()

    below = 2 * z + 2 * xi + core + o
    with scope("Abar"):
        @pl.when(below > 0)
        def _():
            pl.semaphore_wait(barrier, below)

    for k, (peer, upper) in enumerate(near):
        @pl.when(upper == 1)
        def _():
            signal(ready.at[k], peer)

    lowers(lambda zz, xx: signal(s_ready.at[slot(zz, xx)], peer_at(zz, xx)))

    def send(src, dst, ssem, rsem, peer):
        return pltpu.make_async_remote_copy(
            src_ref=src, dst_ref=dst, send_sem=ssem, recv_sem=rsem,
            device_id=peer, device_id_type=MESH)

    def s_copy(zz, xx):
        k = slot(zz, xx)
        return send(s_hbm, all_s.at[z, xi, core], s_send.at[k], s_recv.at[k], peer_at(zz, xx))

    def c_copy(zz, xx, own=False):
        k = slot(zz, xx)
        ref = all_s.at[zz, xx, core]
        return send(s_hbm if own else ref, ref, c_send.at[k], c_recv.at[k], core_peer)

    def t_copy(zz):
        d = xor(zz, z, lines)
        return send(total.at[0], total.at[d], t_send.at[d], t_recv.at[d], peer_at(zz, xi))

    e_copies = [send(part.at[0], part.at[1 + k], e_send.at[k], e_recv.at[k], peer)
                for k, peer in enumerate((peer_at(z, 1 - xi), xc_peer, core_peer))]
    g_copy = send(g_hbm, g_v.at[o], y_send.at[0], y_recv.at[0], y_peer)
    p_copy = send(p_hbm, p_v.at[o], y_send.at[1], y_recv.at[1], y_peer)

    lowers(lambda zz, xx: s_copy(zz, xx).start())

    @pl.when(core == 1)
    def _():
        c_copy(z, xi, True).start()

    @pl.when(o == 1)
    def _():
        g_copy.start()
        p_copy.start()

    load_b.start()
    load_s.start()
    load_g.start()
    load_p.start()

    with scope("Bload"):
        load_f.wait()
        load_d.wait()
    rows = []
    for f in range(fronts):
        row = d_v[front[f] % cols]
        rows.append(jnp.where(front[f] // cols == me, row, jnp.zeros_like(row)))
    part[0] = jnp.concatenate(rows, axis=1)

    @pl.when(xi == 1)
    def _():
        e_copies[0].start()
        e_copies[1].start()

    @pl.when(core == 1)
    def _():
        e_copies[2].start()

    with scope("Cnear"):
        @pl.when(core == 0)
        def _():
            pl.semaphore_wait(ready.at[1], 1)
            e_copies[2].start()
            c_copy(z, xi, True).start()

        @pl.when(o == 0)
        def _():
            pl.semaphore_wait(ready.at[0], 1)
            g_copy.start()
            p_copy.start()

        @pl.when(xi == 0)
        def _():
            pl.semaphore_wait(s_ready.at[slot(z, 1)], 1)
            e_copies[0].start()
            pl.semaphore_wait(ready.at[2], 1)
            e_copies[1].start()
            s_copy(z, 1).start()

    acc[...] = jnp.zeros_like(acc)

    def depart(zz):
        @pl.when(zz > z)
        def _():
            for xx in range(2):
                pl.semaphore_wait(s_ready.at[slot(zz, xx)], 1)
                s_copy(zz, xx).start()

    with scope("Dfar"):
        loop(1, lines, depart)

    with scope("Ediag"):
        for c in e_copies:
            c.wait_recv()
    total[0] = (part[0] + part[1]) + (part[2] + part[3])

    def spread(zz):
        @pl.when(zz != z)
        def _():
            t_copy(zz).start()

    loop(0, lines, spread)

    load_b.wait()
    col0 = blocks[me] * cols
    one, zero = jnp.float32(1), jnp.float32(0)

    def arrive(zz, xx):
        s_copy(zz, xx).wait_recv()
        c_copy(zz, xx).start()

    def product(zz, xx):
        width = 2 * lanes
        start = pl.multiple_of((zz * 2 + xx) * width, width)
        time = (lax.broadcasted_iota(jnp.int32, (1, width), 1) + start) // orb

        def mask(hit):
            return jnp.where(hit, one, zero).astype(jnp.bfloat16)

        left = []
        for t in range(cols):
            keep = mask(time >= col0 + t)
            left += [g_v[h, t, :, pl.ds(start, width)] * keep for h in range(2)]
        right = []
        for f in range(fronts):
            keep = mask(time <= front[f])
            right.append(jnp.concatenate([all_s[zz, xx, 0, f], all_s[zz, xx, 1, f]], axis=1) * keep)
        acc[...] += lax.dot_general(jnp.concatenate(left, axis=0), jnp.concatenate(right, axis=0),
                                    (((1,), (1,)), ((), ())), preferred_element_type=jnp.float32)

    def relay(d):
        zz = xor(z, d, lines)
        with scope("Fz"):
            arrive(zz, xi)
        with scope("Fx"):
            arrive(zz, 1 - xi)

    def use(d):
        zz = xor(z, d, lines)
        c_copy(zz, xi).wait_recv()
        product(zz, xi)
        c_copy(zz, 1 - xi).wait_recv()
        product(zz, 1 - xi)

    with scope("Fx0"):
        arrive(z, 1 - xi)
    loop(1, lines - 1, relay)
    with scope("Gg"):
        load_s.wait()
        load_g.wait()
        g_copy.wait_recv()
    with scope("Huse"):
        loop(0, lines - 2, use)
    with scope("Ilast"):
        loop(lines - 1, lines, relay)
    with scope("Juse"):
        loop(lines - 2, lines, use)

    with jax.named_scope("Kp"):
        load_p.wait()
        p_copy.wait_recv()
    prev = jnp.concatenate(
        [jnp.concatenate([p_v[h, f, t] for f in range(fronts)], axis=1)
         for t in range(cols) for h in range(2)], axis=0)
    combined = acc[...] + prev
    with jax.named_scope("Le"):
        def gather(zz):
            @pl.when(zz != z)
            def _():
                t_copy(zz).wait_recv()

        loop(0, lines, gather)
    both = lax.fori_loop(1, lines, lambda d, v: v + total[d], total[0])
    lane = lax.broadcasted_iota(jnp.int32, both.shape, 1) // orb
    weight = jnp.concatenate([jnp.where(lane == f, both, jnp.zeros_like(both))
                              for f in range(fronts)], axis=0)

    def mine(x):
        blocks_of = [x[k * half:(k + 1) * half] for k in range(x.shape[0] // half)]
        return jnp.concatenate([jnp.where(o == 0, blocks_of[k], blocks_of[k + 1])
                                for k in range(0, len(blocks_of), 2)], axis=0)

    def times(a, b):
        (a0, a1), (b0, b1) = split(a), split(b)
        return lax.dot_general(jnp.concatenate([a0, a1, a0], axis=1), jnp.concatenate([b0, b0, b1], axis=1),
                               (((1,), (1,)), ((), ())), preferred_element_type=jnp.float32)

    g_new = times(mine(combined), weight)
    flipped = times(mine(weight), combined)
    for t in range(cols):
        g_t = g_new[t * half:(t + 1) * half]
        turned = jnp.concatenate([flipped[f * half:(f + 1) * half, t * orb:(t + 1) * orb]
                                  for f in range(fronts)], axis=1)
        s_t = COUPLING * g_t * g_t * turned
        for f in range(fronts):
            out[f, t] = jnp.concatenate([g_t[:, f * orb:(f + 1) * orb], s_t[:, f * orb:(f + 1) * orb]], axis=1)

    with scope("Msend"):
        g_copy.wait_send()
        p_copy.wait_send()
        for c in e_copies:
            c.wait_send()

        def finish(zz):
            @pl.when(zz != z)
            def _():
                t_copy(zz).wait_send()
                s_copy(zz, xi).wait_send()
                s_copy(zz, 1 - xi).wait_send()
                c_copy(zz, xi).wait_send()
                c_copy(zz, 1 - xi).wait_send()

        loop(0, lines, finish)
        s_copy(z, 1 - xi).wait_send()
        c_copy(z, xi, True).wait_send()
        c_copy(z, 1 - xi).wait_send()


def body(lines, g_hist, sigma_hist, diag_inv, previous, block_of_slot, front_pos):
    cols, half, depth = g_hist.shape
    fronts, orb, lanes = sigma_hist.shape
    hbm = pl.BlockSpec(memory_space=pl.ANY)
    dma = pltpu.SemaphoreType.DMA
    regular = pltpu.SemaphoreType.REGULAR
    f32 = jnp.float32
    flops = 2 * cols * orb * depth * orb * fronts
    out = pl.pallas_call(
        functools.partial(kernel, lines),
        out_shape=pltpu.VMEM((fronts, cols, half, 2 * orb), f32),
        in_specs=[hbm] * 6,
        out_specs=pl.BlockSpec(memory_space=pltpu.VMEM),
        scratch_shapes=[
            pltpu.SMEM(block_of_slot.shape, jnp.int32),
            pltpu.SMEM(front_pos.shape, jnp.int32),
            pltpu.VMEM((2,) + g_hist.shape, g_hist.dtype),
            pltpu.VMEM((lines, 2, 2) + sigma_hist.shape, sigma_hist.dtype),
            pltpu.VMEM(diag_inv.shape, f32),
            pltpu.VMEM((2,) + previous.shape, f32),
            pltpu.VMEM((cols * orb, fronts * orb), f32),
            pltpu.VMEM((4, orb, fronts * orb), f32),
            pltpu.VMEM((lines, orb, fronts * orb), f32),
            dma((6,)),
            dma((2 * lines,)), dma((2 * lines,)),
            dma((2 * lines,)), dma((2 * lines,)),
            dma((3,)), dma((3,)),
            dma((lines,)), dma((lines,)),
            dma((2,)), dma((2,)),
            regular((3,)), regular((2 * lines,)),
        ],
        compiler_params=pltpu.CompilerParams(collective_id=0, has_side_effects=True),
        cost_estimate=pl.CostEstimate(flops=flops, bytes_accessed=2 * g_hist.size, transcendentals=0),
    )(block_of_slot, front_pos, g_hist, sigma_hist, diag_inv, previous)
    return out[..., :orb], out[..., orb:]


def solution(mesh):
    lines = mesh.shape["hist"] // 4
    in_specs = (
        P("hist", "orb", None),
        P(None, None, "hist"),
        P("hist", None, None),
        P(None, "hist", "orb", None),
        P(),
        P(),
    )
    out_specs = (P(None, "hist", "orb", None), P(None, "hist", "orb", None))
    return jax.shard_map(functools.partial(body, lines), mesh=mesh, in_specs=in_specs,
                         out_specs=out_specs, check_vma=False)
```

time: 20 us -> 16.8 us (0.84)
  Pallas kernels: 18.5 us -> 15.3 us
    pallas_call x1, Pallas kernels: 18.5 us -> 15.3 us  [body(): pl.pallas_call(functools.partial(kernel, lines), out_shape=pltpu.VMEM((fr...]
where the time goes in v1:
time: 16.8 us; the launch traced here: 16.6 us
  Pallas kernels  15.3 us (91%)
  local copies, waits for them, and re-layouts  0.72 us (4%)
  between operations  0.64 us (4%)
    pallas_call x1, Pallas kernels, body(): pl.pallas_call(functools.partial(kernel, lines), out_shape=pltpu.VMEM((fr...  15.3 us
    slice x1, local copies, waits for them, and re-layouts, body(): return (out[..., :orb], out[..., orb:])  0.72 us

profile of v1, /device:TPU:0, one launch (start us, length us, event | category | flops | bytes accessed | tf_op | source)
XLA Modules:
  0.0 16.6 jit_solution(6757473156493306494)
XLA Ops:
  0.6 15.3 %shard_map.77 = f32[2,2,32,128]{3,2,1,0:T(8,128)S(1)} custom-call(s32[16]{0:T(128)} %blocks_hbm.1, s32[2]{0:T(128)} %front_hbm.1, bf16[2,32,2048]{2,1,0:T(8,128)(2,1)} %g_hbm.1, bf16[2,64,128]{2,1,0:T(8,128)(2,1)} %s_hbm.1, f32[2,64,64]{2,1,0:T(8,128)} %d_hbm.1, f32[2,2,32,64]{3,2,1,0:T(8,128)} %p_hbm.1), custom_call_target="tpu_custom_call" | custom-call | flops 67108864 | bytes 262144 | tf_op jit(solution)/shard_map/pallas_call | solution.py:352
  15.9 0.7 %fusion = (f32[2,2,32,64]{3,2,1,0:T(8,128)}, f32[2,2,32,64]{3,2,1,0:T(8,128)}) fusion(f32[2,2,32,128]{3,2,1,0:T(8,128)S(1)} %shard_map.77), kind=kLoop, calls=%fused_computation | loop fusion | bytes 131072 | tf_op jit(solution)/shard_map/slice | solution.py:378

commit v2 on v1

v2 whole, which is shorter than its diff:
```python
import functools

import jax
import jax.numpy as jnp
from jax import lax
from jax.experimental import pallas as pl
from jax.experimental.pallas import tpu as pltpu
from jax.sharding import PartitionSpec as P

COUPLING = 0.5
MESH = pl.DeviceIdType.MESH


def xor(a, b, size):
    out, bit = 0, 1
    while bit < size:
        out = out + bit * ((a // bit + b // bit) % 2)
        bit *= 2
    return out


def loop(low, high, step):
    if high - low <= 8:
        for i in range(low, high):
            step(i)
    else:
        lax.fori_loop(low, high, lambda i, c: (step(i), c)[1], 0)


def split(x):
    high = x.astype(jnp.bfloat16)
    return high, (x - high.astype(jnp.float32)).astype(jnp.bfloat16)


def kernel(lines, blocks_hbm, front_hbm, g_hbm, s_hbm, d_hbm, p_hbm, out,
           blocks, front, g_v, all_s, d_v, p_v, p_all, acc, col_d, cross_d, sums, sent, sent_rows,
           loc, sends, dc_send, dz_send, x_send, root_send, z_recv, x_recv, c_recv, near_recv, ready):
    cols, half = g_hbm.shape[0], g_hbm.shape[1]
    fronts, orb, lanes = s_hbm.shape
    width = 2 * lanes
    me = lax.axis_index("hist")
    o = lax.axis_index("orb")
    core = me % 2
    xi = (me // 2) % 2
    z = me // 4
    late = lines // 2
    has_rows = z >= late
    first = (z == 0) & (xi == 0)
    beside = (z == 0) & (xi == 1)
    across = (z == lines - 1) & (xi == 1)
    special = jnp.where(z == lines - 1, 0, lines - 1)

    def at(zz, xx, cc):
        return (zz * 2 + xx) * 2 + cc

    def scope(name):
        return jax.named_scope(name)

    y_peer = (me, 1 - o)
    core_peer = (at(z, xi, 1 - core), o)
    x_peer = (at(z, 1 - xi, core), o)
    xc_peer = (at(z, 1 - xi, 1 - core), o)
    near = ((y_peer, o), (core_peer, core), (x_peer, xi), (xc_peer, xi))

    def z_peer(zz):
        return (at(zz, xi, core), o)

    def dist(zz):
        return xor(zz, z, lines)

    barrier = pltpu.get_barrier_semaphore()

    def signal(sem, peer):
        pl.semaphore_signal(sem, inc=1, device_id=peer, device_id_type=MESH)

    def above(step):
        def one(zz):
            @pl.when(zz > z)
            def _():
                step(zz)

        loop(1, lines, one)

    def below(step, low=0):
        def one(zz):
            @pl.when(zz < z)
            def _():
                step(zz)

        loop(low, lines - 1, one)

    for peer, upper in near:
        @pl.when(upper == 0)
        def _():
            signal(barrier, peer)

    above(lambda zz: signal(barrier, z_peer(zz)))

    @pl.when(first)
    def _():
        loop(late, lines, lambda zz: signal(barrier, (at(zz, 1, core), o)))

    load_f = pltpu.make_async_copy(front_hbm, front, loc.at[0])
    load_d = pltpu.make_async_copy(d_hbm, d_v.at[core], loc.at[1])
    load_s = pltpu.make_async_copy(s_hbm, all_s.at[z, xi, core], loc.at[2])
    load_g = pltpu.make_async_copy(g_hbm, g_v.at[o], loc.at[3])
    load_p = pltpu.make_async_copy(p_hbm, p_v, loc.at[4])
    load_b = pltpu.make_async_copy(blocks_hbm, blocks, loc.at[5])
    load_f.start()

    @pl.when(has_rows)
    def _():
        load_d.start()

    earlier = z + 2 * xi + core + o + jnp.where(has_rows, xi, 0)
    with scope("Abar"):
        @pl.when(earlier > 0)
        def _():
            pl.semaphore_wait(barrier, earlier)

    for k, (peer, upper) in enumerate(near):
        @pl.when(upper == 1)
        def _():
            signal(ready.at[k], peer)

    below(lambda zz: signal(ready.at[len(near) + dist(zz) - 1], z_peer(zz)))

    def send(src, dst, rsem, peer, ssem=sends):
        return pltpu.make_async_remote_copy(
            src_ref=src, dst_ref=dst, send_sem=ssem, recv_sem=rsem,
            device_id=peer, device_id_type=MESH)

    def arrived(ref, sem):
        pltpu.make_async_copy(ref, ref, sem).wait()

    def z_copy(zz):
        return send(s_hbm, all_s.at[z, xi, core], z_recv.at[dist(zz) - 1], z_peer(zz))

    def x_copy(zz, own=False, ssem=sends):
        ref = all_s.at[zz, xi, core]
        return send(s_hbm if own else ref, ref, x_recv.at[dist(zz)], x_peer, ssem)

    root_copy = send(s_hbm, all_s.at[z, xi, core], x_recv.at[z], (core, o), root_send)

    def c_copy(zz, xx, own=False):
        ref = all_s.at[zz, xx, core]
        return send(s_hbm if own else ref, ref, c_recv.at[dist(zz)], core_peer)

    def part_of(zz):
        return pl.ds(pl.multiple_of(zz * 2 * width, 2 * width), 2 * width)

    def g_copy(d):
        part = part_of(xor(z, d, lines))
        return send(g_hbm.at[:, :, part], g_v.at[o, :, :, part], near_recv.at[0], y_peer)

    def dz_copy(zz):
        return send(col_d.at[z - late], col_d.at[z - late], near_recv.at[2], z_peer(zz), dz_send)

    droot_copy = send(col_d.at[z - late], cross_d.at[z - late], near_recv.at[5], (core, o), root_send)
    p_copy = send(p_all.at[o], p_all.at[o], near_recv.at[1], y_peer)
    dc_copy = send(d_hbm, d_v.at[core], near_recv.at[4], core_peer, dc_send)
    sum_copies = [send(sums.at[0], sums.at[1 + k], near_recv.at[3], peer, x_send)
                  for k, peer in enumerate((x_peer, xc_peer))]
    core_sum = send(sums.at[4], sums.at[3], near_recv.at[3], core_peer)

    @pl.when(has_rows & (core == 1))
    def _():
        dc_copy.start()

    @pl.when(z == lines - 1)
    def _():
        z_copy(lines - 2).start()
        loop(0, lines - 2, lambda zz: z_copy(zz).start())

        @pl.when(xi == 1)
        def _():
            root_copy.start()

    @pl.when(z < lines - 1)
    def _():
        below(lambda zz: z_copy(zz).start())

    @pl.when(xi == 1)
    def _():
        x_copy(z, True).start()

    @pl.when(core == 1)
    def _():
        c_copy(z, xi, True).start()

    @pl.when(o == 1)
    def _():
        loop(1, lines, lambda d: g_copy(d).start())

    load_s.start()
    load_g.start()
    load_p.start()
    load_b.start()

    @pl.when(core == 0)
    def _():
        with scope("Bcore"):
            pl.semaphore_wait(ready.at[1], 1)

        @pl.when(has_rows)
        def _():
            dc_copy.start()

        c_copy(z, xi, True).start()

    load_f.wait()

    @pl.when(has_rows)
    def _():
        with scope("Bload"):
            load_d.wait()
            dc_copy.wait_recv()
        mine = front[core]
        row = d_v[(mine // cols) % 2, mine % cols]
        row = jnp.where(mine // (2 * cols) == me // 2, row, jnp.zeros_like(row))
        col_d[z - late] = jnp.concatenate([row[:half], row[half:]], axis=1)

        @pl.when(xi == 1)
        def _():
            droot_copy.start()

        below(lambda zz: dz_copy(zz).start())

    with scope("Cnear"):
        @pl.when(o == 0)
        def _():
            pl.semaphore_wait(ready.at[0], 1)
            loop(1, lines, lambda d: g_copy(d).start())

        @pl.when(xi == 0)
        def _():
            pl.semaphore_wait(ready.at[2], 1)
            x_copy(z, True).start()
            pl.semaphore_wait(ready.at[3], 1)

    acc[...] = jnp.zeros_like(acc)

    def depart(zz):
        pl.semaphore_wait(ready.at[len(near) + dist(zz) - 1], 1)
        z_copy(zz).start()

        @pl.when(has_rows)
        def _():
            dz_copy(zz).start()

    with scope("Dfar"):
        above(depart)

    one, zero = jnp.float32(1), jnp.float32(0)

    def mask(hit):
        return jnp.where(hit, one, zero).astype(jnp.bfloat16)

    def product(zz, xx, hs):
        start = pl.multiple_of((zz * 2 + xx) * width, width)
        time = (lax.broadcasted_iota(jnp.int32, (1, width), 1) + start) // orb
        left = []
        for t in range(cols):
            keep = mask(time >= blocks[me] * cols + t)
            left += [g_v[h, t, :, pl.ds(start, width)] * keep for h in hs]
        right = []
        for f in range(fronts):
            keep = mask(time <= front[f])
            right.append(jnp.concatenate([all_s[zz, xx, 0, f], all_s[zz, xx, 1, f]], axis=1) * keep)
        return lax.dot_general(jnp.concatenate(left, axis=0), jnp.concatenate(right, axis=0),
                               (((1,), (1,)), ((), ())), preferred_element_type=jnp.float32)

    def outward(step):
        def both(d):
            @pl.when(z + d < lines)
            def _():
                step(z + d, d)

            @pl.when(z >= d)
            def _():
                step(z - d, d)

        return both

    @outward
    def z_relay(zz, d):
        with scope("Fz"):
            z_copy(zz).wait_recv()
        @pl.when(zz != special)
        def _():
            x_copy(zz).start()

        @pl.when((zz == special) & ~beside)
        def _():
            x_copy(zz, ssem=x_send).start()

        c_copy(zz, xi).start()

    def x_step(zz, d):
        with scope("Gx"):
            x_copy(zz).wait_recv()
        c_copy(zz, 1 - xi).start()

    x_relay = outward(x_step)

    def c_wait(zz):
        arrived(all_s.at[zz, :, 1 - core], c_recv.at[dist(zz)])

    def use(d):
        zz = xor(z, d, lines)
        with scope("Hc"):
            c_wait(zz)
        value = product(zz, xi, range(2)) + product(zz, 1 - xi, range(2))
        acc[...] += value.reshape(acc.shape)

    z_relay(1)
    with scope("Ex0"):
        x_step(z, 0)
    with scope("Eown"):
        load_s.wait()
        load_g.wait()
        load_p.wait()
        load_b.wait()
        c_wait(z)
    start_rows = product(z, xi, (o,)) + product(z, 1 - xi, (o,))
    for t in range(cols):
        prev = jnp.concatenate([p_v[f, t] for f in range(fronts)], axis=1)
        p_all[o, t] = start_rows[t * half:(t + 1) * half] + prev
    p_copy.start()

    loop(2, lines, z_relay)
    x_relay(1)

    with scope("Idz"):
        @pl.when(has_rows)
        def _():
            arrived(col_d.at[pl.ds(0, late - 1)], near_recv.at[2])

        @pl.when(z < late)
        def _():
            arrived(col_d, near_recv.at[2])

    sums[0] = lax.fori_loop(1, late, lambda d, v: v + col_d[d], col_d[0])
    sums[4] = sums[0]

    @pl.when(~beside)
    def _():
        for c in sum_copies:
            c.start()

    @pl.when(first)
    def _():
        arrived(cross_d, near_recv.at[5])
        sums[4] = lax.fori_loop(0, late, lambda d, v: v + cross_d[d], sums[0])
        sums[1] = jnp.zeros_like(sums[1])
        sums[2] = jnp.zeros_like(sums[2])

    core_sum.start()

    loop(2, lines, x_relay)
    with scope("Jg"):
        arrived(g_v.at[1 - o, :, :, pl.ds(0, (lines - 1) * 2 * width)], near_recv.at[0])
    loop(1, lines, use)

    with scope("Kp"):
        p_copy.wait_recv()
    combined = jnp.concatenate([acc[t, h] + p_all[h, t] for t in range(cols) for h in range(2)], axis=0)
    own = jnp.concatenate([acc[t, o] + p_all[o, t] for t in range(cols)], axis=0)
    combined, own = split(combined), split(own)
    with scope("Lw"):
        @pl.when(first)
        def _():
            core_sum.wait_recv()

        @pl.when(~first)
        def _():
            arrived(sums.at[pl.ds(1, 3)], near_recv.at[3])

    same, other = sums[4] + sums[1], sums[3] + sums[2]
    rows = [jnp.where(core == 0, same, other), jnp.where(core == 0, other, same)]
    lane = lax.broadcasted_iota(jnp.int32, (half, fronts * orb), 1) // orb
    blocks_w = []
    for f in range(fronts):
        turned = pltpu.roll(rows[f], orb, 1)
        none = jnp.zeros_like(turned)
        blocks_w.append([jnp.where(lane == f, rows[f] if h == f else turned, none) for h in range(2)])
    weight = split(jnp.concatenate([w for pair in blocks_w for w in pair], axis=0))
    own_weight = split(jnp.concatenate([jnp.where(o == 0, pair[0], pair[1]) for pair in blocks_w], axis=0))

    def times(a, b):
        return lax.dot_general(jnp.concatenate([a[0], a[1], a[0]], axis=1),
                               jnp.concatenate([b[0], b[0], b[1]], axis=1),
                               (((1,), (1,)), ((), ())), preferred_element_type=jnp.float32)

    g_new = times(own, weight)
    flipped = times(own_weight, combined)
    for t in range(cols):
        g_t = g_new[t * half:(t + 1) * half]
        turned = jnp.concatenate([flipped[f * half:(f + 1) * half, t * orb:(t + 1) * orb]
                                  for f in range(fronts)], axis=1)
        s_t = COUPLING * g_t * g_t * turned
        for f in range(fronts):
            out[f, t] = jnp.concatenate([g_t[:, f * orb:(f + 1) * orb], s_t[:, f * orb:(f + 1) * orb]], axis=1)

    with scope("Msend"):
        @pl.when(has_rows)
        def _():
            dc_copy.wait_send()
            arrived(sent_rows, dz_send)

        @pl.when(across)
        def _():
            root_copy.wait_send()

        @pl.when(has_rows & (xi == 1))
        def _():
            droot_copy.wait_send()

        @pl.when(~beside)
        def _():
            arrived(all_s.at[0, 0], x_send)

        arrived(sent, sends)


def body(lines, g_hist, sigma_hist, diag_inv, previous, block_of_slot, front_pos):
    cols, half, depth = g_hist.shape
    fronts, orb, lanes = sigma_hist.shape
    hbm = pl.BlockSpec(memory_space=pl.ANY)
    dma = pltpu.SemaphoreType.DMA
    regular = pltpu.SemaphoreType.REGULAR
    f32 = jnp.float32
    packed = (orb // 2, 2 * orb)
    width = 2 * lanes
    sent = 2 * (4 * lines - 2) * sigma_hist.size + 2 * g_hist.size * (lines - 1) // lines
    sent += 4 * orb * orb + 4 * cols * half * fronts * orb
    flops = 2 * cols * orb * depth * orb * fronts
    out = pl.pallas_call(
        functools.partial(kernel, lines),
        out_shape=pltpu.VMEM((fronts, cols, half, 2 * orb), f32),
        in_specs=[hbm] * 6,
        out_specs=pl.BlockSpec(memory_space=pltpu.VMEM),
        scratch_shapes=[
            pltpu.SMEM(block_of_slot.shape, jnp.int32),
            pltpu.SMEM(front_pos.shape, jnp.int32),
            pltpu.VMEM((2,) + g_hist.shape, g_hist.dtype),
            pltpu.VMEM((lines, 2, 2) + sigma_hist.shape, sigma_hist.dtype),
            pltpu.VMEM((2,) + diag_inv.shape, f32),
            pltpu.VMEM(previous.shape, f32),
            pltpu.VMEM((2, cols, half, fronts * orb), f32),
            pltpu.VMEM((cols, 2, half, fronts * orb), f32),
            pltpu.VMEM((lines // 2,) + packed, f32),
            pltpu.VMEM((lines // 2,) + packed, f32),
            pltpu.VMEM((5,) + packed, f32),
            pltpu.VMEM((sent // width, width // 2), jnp.bfloat16),
            pltpu.VMEM((lines - 1,) + packed, f32),
            dma((6,)), dma, dma, dma, dma, dma,
            dma((lines - 1,)), dma((lines,)), dma((lines,)),
            dma((6,)), regular((3 + lines,)),
        ],
        compiler_params=pltpu.CompilerParams(collective_id=0, has_side_effects=True),
        cost_estimate=pl.CostEstimate(flops=flops, bytes_accessed=2 * g_hist.size, transcendentals=0),
    )(block_of_slot, front_pos, g_hist, sigma_hist, diag_inv, previous)
    return out[..., :orb], out[..., orb:]


def solution(mesh):
    lines = mesh.shape["hist"] // 4
    in_specs = (
        P("hist", "orb", None),
        P(None, None, "hist"),
        P("hist", None, None),
        P(None, "hist", "orb", None),
        P(),
        P(),
    )
    out_specs = (P(None, "hist", "orb", None), P(None, "hist", "orb", None))
    return jax.shard_map(functools.partial(body, lines), mesh=mesh, in_specs=in_specs,
                         out_specs=out_specs, check_vma=False)
```

time: 16.8 us -> 14.9 us (0.89)
  the two profiles are of different devices: /device:TPU:0 before, /device:TPU:9 now
where the time goes in v2:
time: 14.9 us; the launch traced here: 14.6 us
  Pallas kernels  13.3 us (89%)
  local copies, waits for them, and re-layouts  0.72 us (5%)
  between operations  0.64 us (4%)
    pallas_call x1, Pallas kernels, body(): pl.pallas_call(functools.partial(kernel, lines), out_shape=pltpu.VMEM((fr...  13.3 us
    slice x1, local copies, waits for them, and re-layouts, body(): return (out[..., :orb], out[..., orb:])  0.72 us

profile of v2, /device:TPU:9, one launch (start us, length us, event | category | flops | bytes accessed | tf_op | source)
XLA Modules:
  0.0 14.6 jit_solution(2526490191204911035)
XLA Ops:
  0.6 13.3 %shard_map.77 = f32[2,2,32,128]{3,2,1,0:T(8,128)S(1)} custom-call(s32[16]{0:T(128)} %blocks_hbm.1, s32[2]{0:T(128)} %front_hbm.1, bf16[2,32,2048]{2,1,0:T(8,128)(2,1)} %g_hbm.1, bf16[2,64,128]{2,1,0:T(8,128)(2,1)} %s_hbm.1, f32[2,64,64]{2,1,0:T(8,128)} %d_hbm.1, f32[2,2,32,64]{3,2,1,0:T(8,128)} %p_hbm.1), custom_call_target="tpu_custom_call" | custom-call | flops 67108864 | bytes 262144 | tf_op jit(solution)/shard_map/pallas_call | solution.py:438
  13.9 0.7 %fusion = (f32[2,2,32,64]{3,2,1,0:T(8,128)}, f32[2,2,32,64]{3,2,1,0:T(8,128)}) fusion(f32[2,2,32,128]{3,2,1,0:T(8,128)S(1)} %shard_map.77), kind=kLoop, calls=%fused_computation | loop fusion | bytes 131072 | tf_op jit(solution)/shard_map/slice | solution.py:464

commit v3 on v2

--- a/solution.py
+++ b/solution.py
@@ -34,7 +34,7 @@
 
 def kernel(lines, blocks_hbm, front_hbm, g_hbm, s_hbm, d_hbm, p_hbm, out,
            blocks, front, g_v, all_s, d_v, p_v, p_all, acc, col_d, cross_d, sums, sent, sent_rows,
-           loc, sends, dc_send, dz_send, x_send, root_send, z_recv, x_recv, c_recv, near_recv, ready):
+           loc, sends, z_recv, x_recv, c_recv, near_recv, ready):
     cols, half = g_hbm.shape[0], g_hbm.shape[1]
     fronts, orb, lanes = s_hbm.shape
     width = 2 * lanes
@@ -45,9 +45,11 @@
     z = me // 4
     late = lines // 2
     has_rows = z >= late
-    first = (z == 0) & (xi == 0)
-    beside = (z == 0) & (xi == 1)
-    across = (z == lines - 1) & (xi == 1)
+    front_plane = o == 0
+    first = (z == 0) & (xi == 0) & front_plane
+    beside = (z == 0) & (xi == 1) & front_plane
+    across = (z == lines - 1) & (xi == 1) & front_plane
+    aside = has_rows & (xi == 1) & front_plane
     special = jnp.where(z == lines - 1, 0, lines - 1)
 
     def at(zz, xx, cc):
@@ -103,16 +105,16 @@
     load_f = pltpu.make_async_copy(front_hbm, front, loc.at[0])
     load_d = pltpu.make_async_copy(d_hbm, d_v.at[core], loc.at[1])
     load_s = pltpu.make_async_copy(s_hbm, all_s.at[z, xi, core], loc.at[2])
-    load_g = pltpu.make_async_copy(g_hbm, g_v.at[o], loc.at[3])
-    load_p = pltpu.make_async_copy(p_hbm, p_v, loc.at[4])
-    load_b = pltpu.make_async_copy(blocks_hbm, blocks, loc.at[5])
+    load_g = pltpu.make_async_copy(g_hbm, g_v.at[o], loc.at[2])
+    load_p = pltpu.make_async_copy(p_hbm, p_v, loc.at[1])
+    load_b = pltpu.make_async_copy(blocks_hbm, blocks, loc.at[0])
     load_f.start()
 
     @pl.when(has_rows)
     def _():
         load_d.start()
 
-    earlier = z + 2 * xi + core + o + jnp.where(has_rows, xi, 0)
+    earlier = z + 2 * xi + core + o + jnp.where(aside, 1, 0)
     with scope("Abar"):
         @pl.when(earlier > 0)
         def _():
@@ -121,13 +123,13 @@
     for k, (peer, upper) in enumerate(near):
         @pl.when(upper == 1)
         def _():
-            signal(ready.at[k], peer)
-
-    below(lambda zz: signal(ready.at[len(near) + dist(zz) - 1], z_peer(zz)))
-
-    def send(src, dst, rsem, peer, ssem=sends):
+            signal(ready.at[min(k, 2)], peer)
+
+    below(lambda zz: signal(ready.at[2 + dist(zz)], z_peer(zz)))
+
+    def send(src, dst, rsem, peer):
         return pltpu.make_async_remote_copy(
-            src_ref=src, dst_ref=dst, send_sem=ssem, recv_sem=rsem,
+            src_ref=src, dst_ref=dst, send_sem=sends, recv_sem=rsem,
             device_id=peer, device_id_type=MESH)
 
     def arrived(ref, sem):
@@ -136,11 +138,11 @@
     def z_copy(zz):
         return send(s_hbm, all_s.at[z, xi, core], z_recv.at[dist(zz) - 1], z_peer(zz))
 
-    def x_copy(zz, own=False, ssem=sends):
+    def x_copy(zz, own=False):
         ref = all_s.at[zz, xi, core]
-        return send(s_hbm if own else ref, ref, x_recv.at[dist(zz)], x_peer, ssem)
-
-    root_copy = send(s_hbm, all_s.at[z, xi, core], x_recv.at[z], (core, o), root_send)
+        return send(s_hbm if own else ref, ref, x_recv.at[dist(zz)], x_peer)
+
+    root_copy = send(s_hbm, all_s.at[z, xi, core], x_recv.at[z], (core, o))
 
     def c_copy(zz, xx, own=False):
         ref = all_s.at[zz, xx, core]
@@ -154,14 +156,14 @@
         return send(g_hbm.at[:, :, part], g_v.at[o, :, :, part], near_recv.at[0], y_peer)
 
     def dz_copy(zz):
-        return send(col_d.at[z - late], col_d.at[z - late], near_recv.at[2], z_peer(zz), dz_send)
-
-    droot_copy = send(col_d.at[z - late], cross_d.at[z - late], near_recv.at[5], (core, o), root_send)
-    p_copy = send(p_all.at[o], p_all.at[o], near_recv.at[1], y_peer)
-    dc_copy = send(d_hbm, d_v.at[core], near_recv.at[4], core_peer, dc_send)
-    sum_copies = [send(sums.at[0], sums.at[1 + k], near_recv.at[3], peer, x_send)
+        return send(col_d.at[z - late], col_d.at[z - late], near_recv.at[1], z_peer(zz))
+
+    droot_copy = send(col_d.at[z - late], cross_d.at[z - late], near_recv.at[3], (core, o))
+    p_copy = send(p_all.at[o], p_all.at[o], near_recv.at[0], y_peer)
+    dc_copy = send(d_hbm, d_v.at[core], near_recv.at[3], core_peer)
+    sum_copies = [send(sums.at[0], sums.at[1 + k], near_recv.at[2], peer)
                   for k, peer in enumerate((x_peer, xc_peer))]
-    core_sum = send(sums.at[4], sums.at[3], near_recv.at[3], core_peer)
+    core_sum = send(sums.at[4], sums.at[3], near_recv.at[2], core_peer)
 
     @pl.when(has_rows & (core == 1))
     def _():
@@ -172,7 +174,7 @@
         z_copy(lines - 2).start()
         loop(0, lines - 2, lambda zz: z_copy(zz).start())
 
-        @pl.when(xi == 1)
+        @pl.when(across)
         def _():
             root_copy.start()
 
@@ -194,8 +196,6 @@
 
     load_s.start()
     load_g.start()
-    load_p.start()
-    load_b.start()
 
     @pl.when(core == 0)
     def _():
@@ -209,23 +209,27 @@
         c_copy(z, xi, True).start()
 
     load_f.wait()
+    load_b.start()
 
     @pl.when(has_rows)
     def _():
         with scope("Bload"):
             load_d.wait()
             dc_copy.wait_recv()
-        mine = front[core]
-        row = d_v[(mine // cols) % 2, mine % cols]
-        row = jnp.where(mine // (2 * cols) == me // 2, row, jnp.zeros_like(row))
-        col_d[z - late] = jnp.concatenate([row[:half], row[half:]], axis=1)
-
-        @pl.when(xi == 1)
+        rows = []
+        for f in range(fronts):
+            mine = front[f]
+            row = d_v[(mine // cols) % 2, mine % cols, pl.ds(core * half, half)]
+            rows.append(jnp.where(mine // (2 * cols) == me // 2, row, jnp.zeros_like(row)))
+        col_d[z - late] = jnp.concatenate(rows, axis=1)
+
+        @pl.when(aside)
         def _():
             droot_copy.start()
 
         below(lambda zz: dz_copy(zz).start())
 
+    load_p.start()
     with scope("Cnear"):
         @pl.when(o == 0)
         def _():
@@ -234,14 +238,11 @@
 
         @pl.when(xi == 0)
         def _():
-            pl.semaphore_wait(ready.at[2], 1)
+            pl.semaphore_wait(ready.at[2], 2)
             x_copy(z, True).start()
-            pl.semaphore_wait(ready.at[3], 1)
-
-    acc[...] = jnp.zeros_like(acc)
 
     def depart(zz):
-        pl.semaphore_wait(ready.at[len(near) + dist(zz) - 1], 1)
+        pl.semaphore_wait(ready.at[2 + dist(zz)], 1)
         z_copy(zz).start()
 
         @pl.when(has_rows)
@@ -256,19 +257,28 @@
     def mask(hit):
         return jnp.where(hit, one, zero).astype(jnp.bfloat16)
 
-    def product(zz, xx, hs):
-        start = pl.multiple_of((zz * 2 + xx) * width, width)
-        time = (lax.broadcasted_iota(jnp.int32, (1, width), 1) + start) // orb
+    def start_of(zz, xx):
+        return pl.multiple_of((zz * 2 + xx) * width, width)
+
+    def times_of(zz, xx):
+        return (lax.broadcasted_iota(jnp.int32, (1, width), 1) + start_of(zz, xx)) // orb
+
+    def left_of(zz, xx, hs):
         left = []
         for t in range(cols):
-            keep = mask(time >= blocks[me] * cols + t)
-            left += [g_v[h, t, :, pl.ds(start, width)] * keep for h in hs]
+            keep = mask(times_of(zz, xx) >= blocks[me] * cols + t)
+            left += [g_v[h, t, :, pl.ds(start_of(zz, xx), width)] * keep for h in hs]
+        return jnp.concatenate(left, axis=0)
+
+    def right_of(zz, xx):
         right = []
         for f in range(fronts):
-            keep = mask(time <= front[f])
+            keep = mask(times_of(zz, xx) <= front[f])
             right.append(jnp.concatenate([all_s[zz, xx, 0, f], all_s[zz, xx, 1, f]], axis=1) * keep)
-        return lax.dot_general(jnp.concatenate(left, axis=0), jnp.concatenate(right, axis=0),
-                               (((1,), (1,)), ((), ())), preferred_element_type=jnp.float32)
+        return jnp.concatenate(right, axis=0)
+
+    def product(left, right):
+        return lax.dot_general(left, right, (((1,), (1,)), ((), ())), preferred_element_type=jnp.float32)
 
     def outward(step):
         def both(d):
@@ -286,13 +296,9 @@
     def z_relay(zz, d):
         with scope("Fz"):
             z_copy(zz).wait_recv()
-        @pl.when(zz != special)
+        @pl.when((zz != special) | ~beside)
         def _():
             x_copy(zz).start()
-
-        @pl.when((zz == special) & ~beside)
-        def _():
-            x_copy(zz, ssem=x_send).start()
 
         c_copy(zz, xi).start()
 
@@ -306,23 +312,25 @@
     def c_wait(zz):
         arrived(all_s.at[zz, :, 1 - core], c_recv.at[dist(zz)])
 
-    def use(d):
+    def value(d):
         zz = xor(z, d, lines)
+        lefts = [left_of(zz, xx, range(2)) for xx in range(2)]
         with scope("Hc"):
             c_wait(zz)
-        value = product(zz, xi, range(2)) + product(zz, 1 - xi, range(2))
-        acc[...] += value.reshape(acc.shape)
+        return product(lefts[0], right_of(zz, 0)) + product(lefts[1], right_of(zz, 1))
+
+    def use(d):
+        acc[...] += value(d).reshape(acc.shape)
 
     z_relay(1)
     with scope("Ex0"):
         x_step(z, 0)
     with scope("Eown"):
-        load_s.wait()
-        load_g.wait()
+        arrived(sent.at[pl.ds(0, 2 * (s_hbm.size + g_hbm.size) // (2 * lanes))], loc.at[2])
         load_p.wait()
         load_b.wait()
         c_wait(z)
-    start_rows = product(z, xi, (o,)) + product(z, 1 - xi, (o,))
+    start_rows = product(left_of(z, 0, (o,)), right_of(z, 0)) + product(left_of(z, 1, (o,)), right_of(z, 1))
     for t in range(cols):
         prev = jnp.concatenate([p_v[f, t] for f in range(fronts)], axis=1)
         p_all[o, t] = start_rows[t * half:(t + 1) * half] + prev
@@ -334,11 +342,11 @@
     with scope("Idz"):
         @pl.when(has_rows)
         def _():
-            arrived(col_d.at[pl.ds(0, late - 1)], near_recv.at[2])
+            arrived(col_d.at[pl.ds(0, late - 1)], near_recv.at[1])
 
         @pl.when(z < late)
         def _():
-            arrived(col_d, near_recv.at[2])
+            arrived(col_d, near_recv.at[1])
 
     sums[0] = lax.fori_loop(1, late, lambda d, v: v + col_d[d], col_d[0])
     sums[4] = sums[0]
@@ -348,25 +356,34 @@
         for c in sum_copies:
             c.start()
 
+    @pl.when(~first)
+    def _():
+        core_sum.start()
+
+
+    loop(2, lines, x_relay)
+
     @pl.when(first)
     def _():
-        arrived(cross_d, near_recv.at[5])
+        with scope("Icross"):
+            arrived(cross_d, near_recv.at[3])
         sums[4] = lax.fori_loop(0, late, lambda d, v: v + cross_d[d], sums[0])
         sums[1] = jnp.zeros_like(sums[1])
         sums[2] = jnp.zeros_like(sums[2])
-
-    core_sum.start()
-
-    loop(2, lines, x_relay)
+        core_sum.start()
+
     with scope("Jg"):
-        arrived(g_v.at[1 - o, :, :, pl.ds(0, (lines - 1) * 2 * width)], near_recv.at[0])
-    loop(1, lines, use)
-
-    with scope("Kp"):
-        p_copy.wait_recv()
-    combined = jnp.concatenate([acc[t, h] + p_all[h, t] for t in range(cols) for h in range(2)], axis=0)
-    own = jnp.concatenate([acc[t, o] + p_all[o, t] for t in range(cols)], axis=0)
-    combined, own = split(combined), split(own)
+        far = g_hbm.size * (lines - 1) // lines + 2 * p_all.size // 2
+        arrived(sent.at[pl.ds(0, 2 * far // (2 * lanes))], near_recv.at[0])
+    for t in range(cols):
+        for h in range(2):
+            acc[t, h] = p_all[h, t]
+    loop(1, lines - 1, use)
+
+    final = value(lines - 1) + acc[...].reshape(cols * orb, fronts * orb)
+    combined = [final[t * orb:(t + 1) * orb] for t in range(cols)]
+    own = split(jnp.concatenate([jnp.where(o == 0, c[:half], c[half:]) for c in combined], axis=0))
+    turns = split(jnp.concatenate([combined[(t + k) % cols] for k in range(fronts) for t in range(cols)], axis=0))
     with scope("Lw"):
         @pl.when(first)
         def _():
@@ -374,51 +391,51 @@
 
         @pl.when(~first)
         def _():
-            arrived(sums.at[pl.ds(1, 3)], near_recv.at[3])
+            arrived(sums.at[pl.ds(1, 3)], near_recv.at[2])
 
     same, other = sums[4] + sums[1], sums[3] + sums[2]
     rows = [jnp.where(core == 0, same, other), jnp.where(core == 0, other, same)]
+    mine = jnp.where(o == 0, rows[0], rows[1])
     lane = lax.broadcasted_iota(jnp.int32, (half, fronts * orb), 1) // orb
-    blocks_w = []
-    for f in range(fronts):
-        turned = pltpu.roll(rows[f], orb, 1)
-        none = jnp.zeros_like(turned)
-        blocks_w.append([jnp.where(lane == f, rows[f] if h == f else turned, none) for h in range(2)])
-    weight = split(jnp.concatenate([w for pair in blocks_w for w in pair], axis=0))
-    own_weight = split(jnp.concatenate([jnp.where(o == 0, pair[0], pair[1]) for pair in blocks_w], axis=0))
+    none = jnp.zeros_like(mine)
+    weight = split(jnp.concatenate([jnp.where(lane == f, r, none) for f in range(fronts) for r in rows], axis=0))
+    own_weight = split(jnp.concatenate([jnp.where(lane == f, mine, none) for f in range(fronts)], axis=0))
 
     def times(a, b):
         return lax.dot_general(jnp.concatenate([a[0], a[1], a[0]], axis=1),
                                jnp.concatenate([b[0], b[0], b[1]], axis=1),
                                (((1,), (1,)), ((), ())), preferred_element_type=jnp.float32)
 
+    def place(f, t):
+        k = (t - f) % fronts
+        return slice(k * cols * orb, (k + 1) * cols * orb)
+
     g_new = times(own, weight)
-    flipped = times(own_weight, combined)
+    flipped = times(own_weight, turns)
     for t in range(cols):
         g_t = g_new[t * half:(t + 1) * half]
-        turned = jnp.concatenate([flipped[f * half:(f + 1) * half, t * orb:(t + 1) * orb]
-                                  for f in range(fronts)], axis=1)
+        turned = sum(jnp.where(lane == f, flipped[f * half:(f + 1) * half, place(f, t)], none) for f in range(fronts))
         s_t = COUPLING * g_t * g_t * turned
-        for f in range(fronts):
-            out[f, t] = jnp.concatenate([g_t[:, f * orb:(f + 1) * orb], s_t[:, f * orb:(f + 1) * orb]], axis=1)
+        out[0, t] = g_t
+        out[1, t] = s_t
 
     with scope("Msend"):
         @pl.when(has_rows)
         def _():
             dc_copy.wait_send()
-            arrived(sent_rows, dz_send)
+            arrived(sent_rows, sends)
 
         @pl.when(across)
         def _():
             root_copy.wait_send()
 
-        @pl.when(has_rows & (xi == 1))
+        @pl.when(aside)
         def _():
             droot_copy.wait_send()
 
         @pl.when(~beside)
         def _():
-            arrived(all_s.at[0, 0], x_send)
+            arrived(all_s.at[0, 0], sends)
 
         arrived(sent, sends)
 
@@ -454,14 +471,14 @@
             pltpu.VMEM((5,) + packed, f32),
             pltpu.VMEM((sent // width, width // 2), jnp.bfloat16),
             pltpu.VMEM((lines - 1,) + packed, f32),
-            dma((6,)), dma, dma, dma, dma, dma,
+            dma((3,)), dma,
             dma((lines - 1,)), dma((lines,)), dma((lines,)),
-            dma((6,)), regular((3 + lines,)),
+            dma((4,)), regular((2 + lines,)),
         ],
         compiler_params=pltpu.CompilerParams(collective_id=0, has_side_effects=True),
         cost_estimate=pl.CostEstimate(flops=flops, bytes_accessed=2 * g_hist.size, transcendentals=0),
     )(block_of_slot, front_pos, g_hist, sigma_hist, diag_inv, previous)
-    return out[..., :orb], out[..., orb:]
+    return tuple(jnp.stack([out[k, ..., f * orb:(f + 1) * orb] for f in range(fronts)]) for k in range(2))
 
 
 def solution(mesh):

time: 14.9 us -> 14.5 us (0.973)
  other arithmetic: 0 us -> 0.67 us
  local copies, waits for them, and re-layouts: 0.72 us -> 0.08 us
  Pallas kernels: 13.3 us -> 13 us
    another operation x0 -> x1, other arithmetic: none -> 0.67 us  [body(): jnp.stack([out[k, ..., f * orb:(f + 1) * orb] for f in range(fronts)])]
    slice x1, local copies, waits for them, and re-layouts: 0.72 us -> 0.08 us  [body(): out[k, ..., f * orb:(f + 1) * orb]]
    pallas_call x1, Pallas kernels: 13.3 us -> 13 us  [body(): pl.pallas_call(functools.partial(kernel, lines), out_shape=pltpu.VMEM((fr...]
where the time goes in v3:
time: 14.5 us; the launch traced here: 14.4 us
  Pallas kernels  13 us (90%)
  other arithmetic  0.67 us (5%)
  between operations  0.64 us (4%)
    pallas_call x1, Pallas kernels, body(): pl.pallas_call(functools.partial(kernel, lines), out_shape=pltpu.VMEM((fr...  13 us
    another operation x1, other arithmetic, body(): jnp.stack([out[k, ..., f * orb:(f + 1) * orb] for f in range(fronts)])  0.67 us

profile of v3, /device:TPU:9, one launch (start us, length us, event | category | flops | bytes accessed | tf_op | source)
XLA Modules:
  0.0 14.4 jit_solution(14257965618127311144)
XLA Ops:
  0.6 13.0 %shard_map.77 = f32[2,2,32,128]{3,2,1,0:T(8,128)S(1)} custom-call(s32[16]{0:T(128)} %blocks_hbm.1, s32[2]{0:T(128)} %front_hbm.1, bf16[2,32,2048]{2,1,0:T(8,128)(2,1)} %g_hbm.1, bf16[2,64,128]{2,1,0:T(8,128)(2,1)} %s_hbm.1, f32[2,64,64]{2,1,0:T(8,128)} %d_hbm.1, f32[2,2,32,64]{3,2,1,0:T(8,128)} %p_hbm.1), custom_call_target="tpu_custom_call" | custom-call | flops 67108864 | bytes 262144 | tf_op jit(solution)/shard_map/pallas_call | solution.py:455
  13.6 0.1 fusion
  13.7 0.7 %pad_maximum_fusion = (f32[2,2,32,64]{3,2,1,0:T(8,128)}, f32[2,2,32,64]{3,2,1,0:T(8,128)}) fusion(f32[1,2,32,64]{3,2,1,0:T(8,128)S(1)} %get-tuple-element.4, f32[1,2,32,64]{3,2,1,0:T(8,128)S(1)} %get-tuple-element.5, f32[1,2,32,64]{3,2,1,0:T(8,128)S(1)} %get-tuple-element.3, f32[1,2,32,64]{3,2,1,0:T(8,128)S(1)} %get-tuple-element.2), kind=kLoop, calls=%fused_computation | loop fusion | flops 16384 | bytes 131072 | tf_op jit(solution)/shard_map/stack | solution.py:481

commit v4 on v3

--- a/solution.py
+++ b/solution.py
@@ -91,12 +91,12 @@
 
         loop(low, lines - 1, one)
 
+    above(lambda zz: signal(barrier, z_peer(zz)))
+
     for peer, upper in near:
         @pl.when(upper == 0)
         def _():
             signal(barrier, peer)
-
-    above(lambda zz: signal(barrier, z_peer(zz)))
 
     @pl.when(first)
     def _():
@@ -120,13 +120,6 @@
         def _():
             pl.semaphore_wait(barrier, earlier)
 
-    for k, (peer, upper) in enumerate(near):
-        @pl.when(upper == 1)
-        def _():
-            signal(ready.at[min(k, 2)], peer)
-
-    below(lambda zz: signal(ready.at[2 + dist(zz)], z_peer(zz)))
-
     def send(src, dst, rsem, peer):
         return pltpu.make_async_remote_copy(
             src_ref=src, dst_ref=dst, send_sem=sends, recv_sem=rsem,
@@ -181,6 +174,13 @@
     @pl.when(z < lines - 1)
     def _():
         below(lambda zz: z_copy(zz).start())
+
+    for k, (peer, upper) in enumerate(near):
+        @pl.when(upper == 1)
+        def _():
+            signal(ready.at[min(k, 2)], peer)
+
+    below(lambda zz: signal(ready.at[2 + dist(zz)], z_peer(zz)))
 
     @pl.when(xi == 1)
     def _():
@@ -317,7 +317,7 @@
         lefts = [left_of(zz, xx, range(2)) for xx in range(2)]
         with scope("Hc"):
             c_wait(zz)
-        return product(lefts[0], right_of(zz, 0)) + product(lefts[1], right_of(zz, 1))
+        return product(jnp.concatenate(lefts, axis=1), jnp.concatenate([right_of(zz, 0), right_of(zz, 1)], axis=1))
 
     def use(d):
         acc[...] += value(d).reshape(acc.shape)
@@ -325,6 +325,7 @@
     z_relay(1)
     with scope("Ex0"):
         x_step(z, 0)
+    loop(2, 3, z_relay)
     with scope("Eown"):
         arrived(sent.at[pl.ds(0, 2 * (s_hbm.size + g_hbm.size) // (2 * lanes))], loc.at[2])
         load_p.wait()
@@ -336,7 +337,7 @@
         p_all[o, t] = start_rows[t * half:(t + 1) * half] + prev
     p_copy.start()
 
-    loop(2, lines, z_relay)
+    loop(3, lines, z_relay)
     x_relay(1)
 
     with scope("Idz"):

time: 14.5 us -> 14.5 us (level)
  no operation moved by 1% of the time
where the time goes in v4:
time: 14.5 us; the launch traced here: 14.4 us
  Pallas kernels  13 us (90%)
  other arithmetic  0.67 us (5%)
  between operations  0.64 us (4%)
    pallas_call x1, Pallas kernels, body(): pl.pallas_call(functools.partial(kernel, lines), out_shape=pltpu.VMEM((fr...  13 us
    another operation x1, other arithmetic, body(): jnp.stack([out[k, ..., f * orb:(f + 1) * orb] for f in range(fronts)])  0.67 us

profile of v4, /device:TPU:9, one launch (start us, length us, event | category | flops | bytes accessed | tf_op | source)
XLA Modules:
  0.0 14.4 jit_solution(4673474829879096332)
XLA Ops:
  0.6 13.0 %shard_map.77 = f32[2,2,32,128]{3,2,1,0:T(8,128)S(1)} custom-call(s32[16]{0:T(128)} %blocks_hbm.1, s32[2]{0:T(128)} %front_hbm.1, bf16[2,32,2048]{2,1,0:T(8,128)(2,1)} %g_hbm.1, bf16[2,64,128]{2,1,0:T(8,128)(2,1)} %s_hbm.1, f32[2,64,64]{2,1,0:T(8,128)} %d_hbm.1, f32[2,2,32,64]{3,2,1,0:T(8,128)} %p_hbm.1), custom_call_target="tpu_custom_call" | custom-call | flops 67108864 | bytes 262144 | tf_op jit(solution)/shard_map/pallas_call | solution.py:456
  13.6 0.1 fusion
  13.7 0.7 %pad_maximum_fusion = (f32[2,2,32,64]{3,2,1,0:T(8,128)}, f32[2,2,32,64]{3,2,1,0:T(8,128)}) fusion(f32[1,2,32,64]{3,2,1,0:T(8,128)S(1)} %get-tuple-element.4, f32[1,2,32,64]{3,2,1,0:T(8,128)S(1)} %get-tuple-element.5, f32[1,2,32,64]{3,2,1,0:T(8,128)S(1)} %get-tuple-element.3, f32[1,2,32,64]{3,2,1,0:T(8,128)S(1)} %get-tuple-element.2), kind=kLoop, calls=%fused_computation | loop fusion | flops 16384 | bytes 131072 | tf_op jit(solution)/shard_map/stack | solution.py:482

commit v5 on v4

--- a/solution.py
+++ b/solution.py
@@ -48,7 +48,10 @@
     front_plane = o == 0
     first = (z == 0) & (xi == 0) & front_plane
     beside = (z == 0) & (xi == 1) & front_plane
-    across = (z == lines - 1) & (xi == 1) & front_plane
+    direct = front_plane & (core == 0)
+    across = (z == lines - 1) & (xi == 1) & direct
+    turns_in = (z == lines - 1) & (xi == 0)
+    skips = (z < late) & (xi == 1)
     aside = has_rows & (xi == 1) & front_plane
     special = jnp.where(z == lines - 1, 0, lines - 1)
 
@@ -136,6 +139,11 @@
         return send(s_hbm if own else ref, ref, x_recv.at[dist(zz)], x_peer)
 
     root_copy = send(s_hbm, all_s.at[z, xi, core], x_recv.at[z], (core, o))
+
+    def turn_copy(zz):
+        ref = all_s.at[lines - 1, 1, core]
+        return send(ref, ref, x_recv.at[xor(zz, lines - 1, lines)], z_peer(zz))
+
 
     def c_copy(zz, xx, own=False):
         ref = all_s.at[zz, xx, core]
@@ -296,7 +304,7 @@
     def z_relay(zz, d):
         with scope("Fz"):
             z_copy(zz).wait_recv()
-        @pl.when((zz != special) | ~beside)
+        @pl.when((zz != special) | ~skips)
         def _():
             x_copy(zz).start()
 
@@ -325,6 +333,15 @@
     z_relay(1)
     with scope("Ex0"):
         x_step(z, 0)
+
+    @pl.when(turns_in)
+    def _():
+        @pl.when(~direct)
+        def _():
+            turn_copy(0).start()
+
+        loop(1, late, lambda zz: turn_copy(zz).start())
+
     loop(2, 3, z_relay)
     with scope("Eown"):
         arrived(sent.at[pl.ds(0, 2 * (s_hbm.size + g_hbm.size) // (2 * lanes))], loc.at[2])
@@ -426,17 +443,29 @@
             dc_copy.wait_send()
             arrived(sent_rows, sends)
 
+        @pl.when(turns_in)
+        def _():
+            @pl.when(~direct)
+            def _():
+                turn_copy(0).wait_send()
+
+            arrived(all_s.at[pl.ds(0, late - 1), 0, 0], sends)
+
         @pl.when(across)
         def _():
             root_copy.wait_send()
 
+        @pl.when(~skips)
+        def _():
+            arrived(all_s.at[0, 0, 0], sends)
+
         @pl.when(aside)
         def _():
             droot_copy.wait_send()
 
         @pl.when(~beside)
         def _():
-            arrived(all_s.at[0, 0], sends)
+            arrived(all_s.at[0, 0, 0], sends)
 
         arrived(sent, sends)
 

time: 14.5 us -> 14.2 us (0.979)
  Pallas kernels: 13 us -> 12.7 us
    pallas_call x1, Pallas kernels: 13 us -> 12.7 us  [body(): pl.pallas_call(functools.partial(kernel, lines), out_shape=pltpu.VMEM((fr...]
where the time goes in v5:
time: 14.2 us; the launch traced here: 14.1 us
  Pallas kernels  12.7 us (89%)
  other arithmetic  0.67 us (5%)
  between operations  0.64 us (5%)
    pallas_call x1, Pallas kernels, body(): pl.pallas_call(functools.partial(kernel, lines), out_shape=pltpu.VMEM((fr...  12.7 us
    another operation x1, other arithmetic, body(): jnp.stack([out[k, ..., f * orb:(f + 1) * orb] for f in range(fronts)])  0.67 us

profile of v5, /device:TPU:9, one launch (start us, length us, event | category | flops | bytes accessed | tf_op | source)
XLA Modules:
  0.0 14.1 jit_solution(2887061677274091283)
XLA Ops:
  0.6 12.7 %shard_map.77 = f32[2,2,32,128]{3,2,1,0:T(8,128)S(1)} custom-call(s32[16]{0:T(128)} %blocks_hbm.1, s32[2]{0:T(128)} %front_hbm.1, bf16[2,32,2048]{2,1,0:T(8,128)(2,1)} %g_hbm.1, bf16[2,64,128]{2,1,0:T(8,128)(2,1)} %s_hbm.1, f32[2,64,64]{2,1,0:T(8,128)} %d_hbm.1, f32[2,2,32,64]{3,2,1,0:T(8,128)} %p_hbm.1), custom_call_target="tpu_custom_call" | custom-call | flops 67108864 | bytes 262144 | tf_op jit(solution)/shard_map/pallas_call | solution.py:485
  13.3 0.1 fusion
  13.4 0.7 %pad_maximum_fusion = (f32[2,2,32,64]{3,2,1,0:T(8,128)}, f32[2,2,32,64]{3,2,1,0:T(8,128)}) fusion(f32[1,2,32,64]{3,2,1,0:T(8,128)S(1)} %get-tuple-element.4, f32[1,2,32,64]{3,2,1,0:T(8,128)S(1)} %get-tuple-element.5, f32[1,2,32,64]{3,2,1,0:T(8,128)S(1)} %get-tuple-element.3, f32[1,2,32,64]{3,2,1,0:T(8,128)S(1)} %get-tuple-element.2), kind=kLoop, calls=%fused_computation | loop fusion | flops 16384 | bytes 131072 | tf_op jit(solution)/shard_map/stack | solution.py:511

commit v6 on v5

--- a/solution.py
+++ b/solution.py
@@ -355,28 +355,37 @@
     p_copy.start()
 
     loop(3, lines, z_relay)
+    def reduce_rows():
+        with scope("Idz"):
+            @pl.when(has_rows)
+            def _():
+                arrived(col_d.at[pl.ds(0, late - 1)], near_recv.at[1])
+
+            @pl.when(z < late)
+            def _():
+                arrived(col_d, near_recv.at[1])
+
+        sums[0] = lax.fori_loop(1, late, lambda d, v: v + col_d[d], col_d[0])
+        sums[4] = sums[0]
+
+        @pl.when(~beside)
+        def _():
+            for c in sum_copies:
+                c.start()
+
+        @pl.when(~first)
+        def _():
+            core_sum.start()
+
+    @pl.when(has_rows)
+    def _():
+        reduce_rows()
+
     x_relay(1)
 
-    with scope("Idz"):
-        @pl.when(has_rows)
-        def _():
-            arrived(col_d.at[pl.ds(0, late - 1)], near_recv.at[1])
-
-        @pl.when(z < late)
-        def _():
-            arrived(col_d, near_recv.at[1])
-
-    sums[0] = lax.fori_loop(1, late, lambda d, v: v + col_d[d], col_d[0])
-    sums[4] = sums[0]
-
-    @pl.when(~beside)
-    def _():
-        for c in sum_copies:
-            c.start()
-
-    @pl.when(~first)
-    def _():
-        core_sum.start()
+    @pl.when(~has_rows)
+    def _():
+        reduce_rows()
 
 
     loop(2, lines, x_relay)

time: 14.2 us -> 14.2 us (level)
  no operation moved by 1% of the time
where the time goes in v6:
time: 14.2 us; the launch traced here: 14.1 us
  Pallas kernels  12.7 us (89%)
  other arithmetic  0.67 us (5%)
  between operations  0.64 us (5%)
    pallas_call x1, Pallas kernels, body(): pl.pallas_call(functools.partial(kernel, lines), out_shape=pltpu.VMEM((fr...  12.7 us
    another operation x1, other arithmetic, body(): jnp.stack([out[k, ..., f * orb:(f + 1) * orb] for f in range(fronts)])  0.67 us

profile of v6, /device:TPU:9, one launch (start us, length us, event | category | flops | bytes accessed | tf_op | source)
XLA Modules:
  0.0 14.1 jit_solution(927862172007119271)
XLA Ops:
  0.6 12.7 %shard_map.77 = f32[2,2,32,128]{3,2,1,0:T(8,128)S(1)} custom-call(s32[16]{0:T(128)} %blocks_hbm.1, s32[2]{0:T(128)} %front_hbm.1, bf16[2,32,2048]{2,1,0:T(8,128)(2,1)} %g_hbm.1, bf16[2,64,128]{2,1,0:T(8,128)(2,1)} %s_hbm.1, f32[2,64,64]{2,1,0:T(8,128)} %d_hbm.1, f32[2,2,32,64]{3,2,1,0:T(8,128)} %p_hbm.1), custom_call_target="tpu_custom_call" | custom-call | flops 67108864 | bytes 262144 | tf_op jit(solution)/shard_map/pallas_call | solution.py:494
  13.3 0.1 fusion
  13.4 0.7 %pad_maximum_fusion = (f32[2,2,32,64]{3,2,1,0:T(8,128)}, f32[2,2,32,64]{3,2,1,0:T(8,128)}) fusion(f32[1,2,32,64]{3,2,1,0:T(8,128)S(1)} %get-tuple-element.4, f32[1,2,32,64]{3,2,1,0:T(8,128)S(1)} %get-tuple-element.5, f32[1,2,32,64]{3,2,1,0:T(8,128)S(1)} %get-tuple-element.3, f32[1,2,32,64]{3,2,1,0:T(8,128)S(1)} %get-tuple-element.2), kind=kLoop, calls=%fused_computation | loop fusion | flops 16384 | bytes 131072 | tf_op jit(solution)/shard_map/stack | solution.py:520

commit v7 on v6

--- a/solution.py
+++ b/solution.py
@@ -251,11 +251,11 @@
 
     def depart(zz):
         pl.semaphore_wait(ready.at[2 + dist(zz)], 1)
+        @pl.when(has_rows)
+        def _():
+            dz_copy(zz).start()
+
         z_copy(zz).start()
-
-        @pl.when(has_rows)
-        def _():
-            dz_copy(zz).start()
 
     with scope("Dfar"):
         above(depart)
@@ -304,11 +304,11 @@
     def z_relay(zz, d):
         with scope("Fz"):
             z_copy(zz).wait_recv()
+        c_copy(zz, xi).start()
+
         @pl.when((zz != special) | ~skips)
         def _():
             x_copy(zz).start()
-
-        c_copy(zz, xi).start()
 
     def x_step(zz, d):
         with scope("Gx"):

time: 14.2 us -> 14.2 us (level)
  no operation moved by 1% of the time
where the time goes in v7:
time: 14.2 us; the launch traced here: 14.1 us
  Pallas kernels  12.7 us (89%)
  other arithmetic  0.67 us (5%)
  between operations  0.64 us (5%)
    pallas_call x1, Pallas kernels, body(): pl.pallas_call(functools.partial(kernel, lines), out_shape=pltpu.VMEM((fr...  12.7 us
    another operation x1, other arithmetic, body(): jnp.stack([out[k, ..., f * orb:(f + 1) * orb] for f in range(fronts)])  0.67 us

profile of v7, /device:TPU:9, one launch (start us, length us, event | category | flops | bytes accessed | tf_op | source)
XLA Modules:
  0.0 14.1 jit_solution(17345341347567280805)
XLA Ops:
  0.6 12.7 %shard_map.77 = f32[2,2,32,128]{3,2,1,0:T(8,128)S(1)} custom-call(s32[16]{0:T(128)} %blocks_hbm.1, s32[2]{0:T(128)} %front_hbm.1, bf16[2,32,2048]{2,1,0:T(8,128)(2,1)} %g_hbm.1, bf16[2,64,128]{2,1,0:T(8,128)(2,1)} %s_hbm.1, f32[2,64,64]{2,1,0:T(8,128)} %d_hbm.1, f32[2,2,32,64]{3,2,1,0:T(8,128)} %p_hbm.1), custom_call_target="tpu_custom_call" | custom-call | flops 67108864 | bytes 262144 | tf_op jit(solution)/shard_map/pallas_call | solution.py:494
  13.3 0.1 fusion
  13.4 0.7 %pad_maximum_fusion = (f32[2,2,32,64]{3,2,1,0:T(8,128)}, f32[2,2,32,64]{3,2,1,0:T(8,128)}) fusion(f32[1,2,32,64]{3,2,1,0:T(8,128)S(1)} %get-tuple-element.4, f32[1,2,32,64]{3,2,1,0:T(8,128)S(1)} %get-tuple-element.5, f32[1,2,32,64]{3,2,1,0:T(8,128)S(1)} %get-tuple-element.3, f32[1,2,32,64]{3,2,1,0:T(8,128)S(1)} %get-tuple-element.2), kind=kLoop, calls=%fused_computation | loop fusion | flops 16384 | bytes 131072 | tf_op jit(solution)/shard_map/stack | solution.py:520
